TPU v7x, 8 devices: a whole 2x2x1 slice. The times are simulated.
8 devices in a mesh: dp: 2 (over y, z), tp: 4 (over x, core).
Axes of the slice: x: 2, y: 2, z: 1, core: 2. Of those that a mesh axis runs over, the one named last changes fastest.
Arguments:
- x: bfloat16 [4096, 1024], P('dp'), parts along dimension 0
- dy: bfloat16 [4096, 1024], P('dp'), parts along dimension 0
- gate: bfloat16 [4096, 3072], P('dp', 'tp'), parts along dimension 0
- up: bfloat16 [4096, 3072], P('dp', 'tp'), parts along dimension 0
- w_gate: bfloat16 [1024, 3072], P(None, 'tp')
- w_up: bfloat16 [1024, 3072], P(None, 'tp')
- w_down: bfloat16 [3072, 1024], P('tp')
Outputs:
- output 1: bfloat16 [4096, 1024], P('dp'), parts along dimension 0
- output 2: bfloat16 [2048, 3072], P('dp', 'tp'), parts along dimension 0
- output 3: bfloat16 [2048, 3072], P('dp', 'tp'), parts along dimension 0
- output 4: bfloat16 [6144, 1024], P(('dp', 'tp')), parts along dimension 0
There are 2 independent parts. A program takes and returns all parts, laid end to end along the dimension named above; an argument that names none is the same for every part.
All inputs are finite; a program needn't handle non-finite values.
Results may differ from a plain program's by a relative error of at most 0.012.
Values are sent between devices in bfloat16 or wider.
A program may use at most 2 GiB of HBM per device.

v0:
```python
import types

import jax
import jax.numpy as jnp
from jax import lax
from jax.experimental import pallas as pl
from jax.experimental.pallas import tpu as pltpu
from jax.sharding import PartitionSpec as P

MESH = pl.DeviceIdType.MESH
F32, BF16 = jnp.float32, jnp.bfloat16
C = 256
SMALL, RS, RB = 2, 64, 128
EARLY, LAST = 1, 4


def dot_t(a, b):
    return lax.dot_general(a, b, (((1,), (1,)), ((), ())), preferred_element_type=F32)


def dot(a, b):
    return lax.dot_general(a, b, (((1,), (0,)), ((), ())), preferred_element_type=F32)


def tile(n, start=0):
    return slice(start + n * C, start + (n + 1) * C)


def kernel(
    x_h, dy_h, gate_h, up_h, wg_h, wu_h, wd_h,
    dx, dwg, dwu, dwd,
    xv, acts, wgu, wd, dgu, hid, xt,
    own_s, tsend_s, trecv_s, psend_s, precv_s, own_b, tsend_b, trecv_b, psend_b, precv_b, extra,
    load_sem, sent, landed, term_sem, part_sem, final_sem, extra_sem,
):
    rows, d = xv.shape
    f = wd.shape[0]
    half = rows // 2
    dyv, gv, uv = acts.at[:, 0:d], acts.at[:, d : d + f], acts.at[:, d + f : d + 2 * f]
    me = lax.axis_index("tp")
    chip, core = me // 2, me % 2
    partner, peer, across = chip * 2 + (1 - core), (1 - chip) * 2 + core, (1 - chip) * 2 + (1 - core)
    nb = (half - SMALL * 2 * RS) // (2 * RB)
    small = types.SimpleNamespace(
        r=RS, off=0, n=SMALL, at=0, own=own_s, tsend=tsend_s, trecv=trecv_s, psend=psend_s, precv=precv_s
    )
    big = types.SimpleNamespace(
        r=RB, off=SMALL * 2 * RS, n=nb, at=SMALL, own=own_b, tsend=tsend_b, trecv=trecv_b, psend=psend_b, precv=precv_b
    )

    def base(q, e):
        owner = lax.rem(chip + 1 + e // q.n, 2)
        return pl.multiple_of(owner * half + q.off + lax.rem(e, q.n) * (2 * q.r), 2 * RS)

    def block(q, e, k):
        return pl.ds(pl.multiple_of(base(q, e) + k * q.r, RS), q.r)

    def local(src, dst, sem):
        return pltpu.make_async_copy(src, dst, load_sem.at[sem])

    def load(q, e, sem):
        r = pl.ds(base(q, e), 2 * q.r)
        return [local(src.at[r], dst.at[r], sem) for src, dst in ((dy_h, dyv), (gate_h, gv), (up_h, uv))]

    def all_of(ref, sem):
        return pltpu.make_async_copy(ref, ref, sem)

    def remote(src, dst, send, recv, to):
        return pltpu.make_async_remote_copy(
            src_ref=src, dst_ref=dst, send_sem=send, recv_sem=recv, device_id={"tp": to}, device_id_type=MESH
        )

    def term_copy(q, e, cols=slice(None), n=0):
        recv = term_sem.at[2 * (2 * q.at + e) + n]
        return remote(q.tsend.at[e, :, cols], q.trecv.at[e, :, cols], sent.at[0], recv, partner)

    def part_copy(q, e, cols=slice(None)):
        return remote(q.psend.at[e, :, cols], q.precv.at[e, :, cols], sent.at[1], part_sem.at[q.at + e], peer)

    def extra_copy():
        return remote(tsend_s.at[0, :, tile(0)], extra, sent.at[0], extra_sem, across)

    def final_copy(q, j):
        r = block(q, q.n + j, core)
        return remote(dx.at[r], dx.at[r], sent.at[2], final_sem.at[q.at + j], peer)

    def core_copy(r):
        return remote(dx.at[r], dx.at[r], sent.at[3], landed, partner)

    def start(copies):
        for c in copies:
            c.start()

    def hidden_tile(q, e, n, dyb):
        dh = dot_t(dyb, wd[tile(n), :])
        for part, k in ((dh[: q.r], 1 - core), (dh[q.r :], core)):
            r = block(q, e, k)
            g, u = gv[r, tile(n)].astype(F32), uv[r, tile(n)].astype(F32)
            sig = jax.nn.sigmoid(g)
            act = g * sig
            hid[r, tile(n)] = (act * u).astype(BF16)
            dgu[r, tile(n)] = ((part * u) * (sig + act * (1.0 - sig))).astype(BF16)
            dgu[r, tile(n, f)] = (part * act).astype(BF16)

    def both(ref, q, e):
        return jnp.concatenate([ref[block(q, e, 1 - core), :], ref[block(q, e, core), :]], axis=0)

    def hidden_part(q, e):
        dyb = both(dyv, q, e)
        for n in range(f // C):
            hidden_tile(q, e, n, dyb)

    def term_tile(q, e, n, lhs):
        t = dot_t(lhs, wgu[tile(n), :])
        q.tsend[e, :, tile(n)] = t[: q.r].astype(BF16)
        q.own[e, :, tile(n)] = t[q.r :]

    def term_part(q, e):
        lhs = both(dgu, q, e)
        for n in range(d // C):
            term_tile(q, e, n, lhs)
        term_copy(q, e).start()

    def chip_sum(q, e, theirs, cols=slice(None), n=0):
        term_copy(q, e, cols, n).wait_recv()
        s = q.own[e, :, cols] + q.trecv[e, :, cols].astype(F32)
        if theirs:
            q.psend[e, :, cols] = s.astype(BF16)
            part_copy(q, e, cols).start()
        else:
            q.own[e, :, cols] = s

    def finish(q, j):
        part_copy(q, j).wait_recv()
        r = block(q, q.n + j, core)
        total = q.own[q.n + j] + q.precv[j].astype(F32)
        if q is small and j == 0:
            extra_copy().wait_recv()
            dx[r, C:] = total[:, C:].astype(BF16)
            dx[r, :C] = (total[:, :C] + extra[...].astype(F32)).astype(BF16)
        else:
            dx[r, :] = total.astype(BF16)
        if q is big and j == 0:
            final_copy(q, j).start()
        else:

            @pl.when(core != EARLY)
            def _():
                final_copy(q, j).start()

        core_copy(r).start()

    def pass_on(q, j):
        final_copy(q, j).wait_recv()
        core_copy(block(q, j, core)).start()

    def grad_x(m):
        r = pl.ds(pl.multiple_of(m * C, C), C)
        xt[...] = xv[:, r].T
        for n in range(f // C):
            dwg[r, tile(n)] = dot(xt[...], dgu[:, tile(n)]).astype(BF16)
            dwu[r, tile(n)] = dot(xt[...], dgu[:, tile(n, f)]).astype(BF16)

    def grad_h(m):
        r = pl.ds(pl.multiple_of(m * C, C), C)
        xt[...] = hid[:, r].T
        for n in range(d // C):
            dwd[r, tile(n)] = dot(xt[...], dyv[:, tile(n)]).astype(BF16)

    nf, nd = f // C, d // C
    w_sem, first_rows, gu, second_rows, rest, x_sem = 0, 1, 2, 4, 5, 6
    first = load(small, 0, first_rows)
    wds = [local(wd_h.at[tile(n)], wd.at[tile(n)], w_sem) for n in range(nf)]
    start(first[:1] + wds[:1] + first[1:] + wds[1:])
    for n in range(nd):
        start([local(w.at[tile(n)], wgu.at[tile(n), c * f : (c + 1) * f], gu + n // 2) for c, w in enumerate((wg_h, wu_h))])
    start(load(small, 1, second_rows))
    for e in range(2 * nb):
        start(load(big, e, rest))
    for e in range(SMALL, 2 * SMALL):
        start(load(small, e, rest))
    x_copy = local(x_h, xv, x_sem)
    start([x_copy])

    barrier = pltpu.get_barrier_semaphore()
    for to in (partner, peer, across):
        pl.semaphore_signal(barrier, inc=1, device_id={"tp": to}, device_id_type=MESH)

    all_of(acts.at[pl.ds(base(small, 0), 2 * RS)], load_sem.at[first_rows]).wait()
    all_of(wd, load_sem.at[w_sem]).wait()
    hidden_part(small, 0)
    pl.semaphore_wait(barrier, 3)
    halves = [slice(n * (d // 2), (n + 1) * (d // 2)) for n in range(2)]

    def halves_of_term(q, e):
        lhs = both(dgu, q, e)
        for n in range(2):
            if q is small and e == 0:
                all_of(wgu.at[halves[n]], load_sem.at[gu + n]).wait()
            for m in range(nd // 2):
                term_tile(q, e, n * (nd // 2) + m, lhs)
            cols = halves[n]
            if q is small and e == 0 and n == 0:
                psend_s[0, :, tile(0)] = own_s[0, :, tile(0)].astype(BF16)
                part_copy(small, 0, tile(0)).start()
                extra_copy().start()
                cols = rest_cols
            term_copy(q, e, cols, n).start()

    rest_cols = slice(C, d // 2)
    halves_of_term(small, 0)
    all_of(acts.at[pl.ds(base(small, 1), 2 * RS)], load_sem.at[second_rows]).wait()
    hidden_part(small, 1)
    chip_sum(small, 0, True, rest_cols, 0)
    chip_sum(small, 0, True, halves[1], 1)
    halves_of_term(small, 1)
    chip_sum(small, 1, True, halves[0], 0)
    all_of(acts.at[0 : rows - SMALL * 2 * RS], load_sem.at[rest]).wait()
    hidden_part(big, 0)
    chip_sum(small, 1, True, halves[1], 1)
    halves_of_term(big, 0)

    @pl.loop(1, 2 * nb)
    def _(e):
        hidden_part(big, e)

        @pl.when(e == 1)
        def _():
            for n in range(2):
                chip_sum(big, 0, True, halves[n], n)

        term_part(big, e)

        @pl.when((e > 1) & (e <= nb))
        def _():
            chip_sum(big, e - 1, True)

        @pl.when(e > nb)
        def _():
            chip_sum(big, e - 1, False)

    for e in range(SMALL, 2 * SMALL):
        hidden_part(small, e)
        term_part(small, e)
        if e == SMALL:
            chip_sum(big, 2 * nb - 1, False)
        else:
            chip_sum(small, e - 1, False)

    x_copy.wait()
    finish(big, 0)
    chip_sum(small, 2 * SMALL - 1, False)
    for j in range(SMALL):
        finish(small, j)
    for j in range(1, nb - 1):
        finish(big, j)

    @pl.loop(0, d // C)
    def _(m):
        grad_x(m)

    finish(big, nb - 1)

    @pl.loop(0, f // C)
    def _(m):
        grad_h(m)

        @pl.when(m == f // C - 2)
        def _():
            pass_on(big, 0)

    ahead = RB
    all_of(dx.at[0:half], sent.at[0]).wait()
    all_of(dx.at[0 : half // 2], sent.at[1]).wait()
    all_of(dx.at[0 : half // 2 + ahead], sent.at[3]).wait()
    all_of(dx.at[0 : half // 2 + ahead], landed).wait()

    @pl.when(core == EARLY)
    def _():
        all_of(dx.at[0:ahead], sent.at[2]).wait()

    @pl.when(core != EARLY)
    def _():
        for q in (small, big):
            for j in range(1 if q is big else 0, q.n):
                final_copy(q, j).wait_recv()
        all_of(dx.at[0 : half // 2], sent.at[2]).wait()


def rest_kernel(_, dx, recv, direct, ready, sent, landed):
    half = dx.shape[0] // 2
    me = lax.axis_index("tp")
    chip, core = me // 2, me % 2
    partner, peer, across = chip * 2 + (1 - core), (1 - chip) * 2 + core, (1 - chip) * 2 + (1 - core)
    big = [(SMALL * 2 * RS + j * 2 * RB, RB, 0, RB) for j in range(1, (half - SMALL * 2 * RS) // (2 * RB))]
    small = [(j * 2 * RS, RS, 0, RS) for j in range(SMALL - 1)]
    last = [((SMALL - 1) * 2 * RS, RS, n * RS // LAST, RS // LAST) for n in range(LAST)]
    pieces = big + small + last

    def rows(owner, piece):
        at, r, off, size = piece
        return pl.ds(pl.multiple_of(owner * half + at + core * r + off, size), size)

    def copy(r, send, recv, to):
        return pltpu.make_async_remote_copy(
            src_ref=dx.at[r], dst_ref=dx.at[r], send_sem=send, recv_sem=recv, device_id={"tp": to}, device_id_type=MESH
        )

    def final_copy(n):
        return copy(rows(chip, pieces[n]), sent.at[0], recv.at[n], peer)

    def core_copy(n):
        return copy(rows(1 - chip, pieces[n]), sent.at[1], landed, partner)

    end = len(pieces) - 1
    direct_copy = copy(rows(chip, pieces[end]), sent.at[0], direct, across)

    def all_of(n, sem):
        return pltpu.make_async_copy(dx.at[0:n], dx.at[0:n], sem)

    size = pieces[end][3]
    passes = half // 2 - RB
    barrier = pltpu.get_barrier_semaphore()

    @pl.when(core == EARLY)
    def _():
        for to in (peer, partner, across):
            pl.semaphore_signal(barrier, inc=1, device_id={"tp": to}, device_id_type=MESH)

    pl.semaphore_wait(barrier, 1 + lax.rem(core + EARLY, 2))

    @pl.when(core == EARLY)
    def _():
        for n in range(len(pieces)):
            final_copy(n).start()
        pl.semaphore_wait(ready, 2)
        direct_copy.start()
        for n in range(len(pieces)):
            final_copy(n).wait_recv()
            if n < end:
                core_copy(n).start()
        all_of(passes + size, sent.at[0]).wait()
        all_of(passes - size, sent.at[1]).wait()
        all_of(passes, landed).wait()

    @pl.when(core != EARLY)
    def _():
        for to in (partner, across):
            pl.semaphore_signal(ready, inc=1, device_id={"tp": to}, device_id_type=MESH)
        for n in range(len(pieces)):
            core_copy(n).start()
        all_of(passes, sent.at[1]).wait()
        all_of(passes - size, landed).wait()
        direct_copy.wait_recv()


def start_all(pairs, sem):
    copies = [pltpu.make_async_copy(a, b, sem) for a, b in pairs]
    for c in copies:
        c.start()
    return copies


def wait_all(copies):
    for c in copies:
        c.wait()


def rows_of(dx):
    half = dx.shape[0] // 2
    chip = lax.axis_index("tp") // 2
    first = SMALL * 2 * RS
    own = [(chip * half + n * (half // 2), half // 2) for n in range(2)]
    theirs = (1 - chip) * half
    steps = [(theirs + n * 2 * RS, RS) for n in range(SMALL)]
    steps += [(theirs + n, RB) for n in range(first + 2 * RB, half, 2 * RB)]

    def slices(parts):
        return [pl.ds(pl.multiple_of(at, RS), size) for at, size in parts]

    late, early = ([(at + k * size, size) for at, size in steps] for k in (1 - EARLY, EARLY))
    return slices(own + [(theirs + first, 2 * RB)]), slices(late), slices(early)


def write_most(dx_v, dwg_v, dwu_v, dwd_v, _, dx, dwg, dwu, dwd, sem):
    done, late, _ = rows_of(dx)
    pairs = [(dx_v.at[r], dx.at[r]) for r in done]
    for src, dst in ((dwg_v, dwg), (dwu_v, dwu), (dwd_v, dwd)):
        n = src.shape[0] // 2
        pairs += [(src.at[r], dst.at[r]) for r in (pl.ds(0, n), pl.ds(n, n))]
    copies = start_all(pairs, sem)

    @pl.when(lax.rem(lax.axis_index("tp"), 2) != EARLY)
    def _():
        wait_all(start_all([(dx_v.at[r], dx.at[r]) for r in late], sem))

    wait_all(copies)


def write_late(dx_v, _, dx, sem):
    _, late, early = rows_of(dx)
    copies = start_all([(dx_v.at[r], dx.at[r]) for r in early], sem)

    @pl.when(lax.rem(lax.axis_index("tp"), 2) == EARLY)
    def _():
        wait_all(start_all([(dx_v.at[r], dx.at[r]) for r in late], sem))

    wait_all(copies)


def solution(mesh):
    def step(x, dy, gate, up, w_gate, w_up, w_down):
        rows, d = x.shape
        f = gate.shape[1]
        nb = (rows // 2 - SMALL * 2 * RS) // (2 * RB)
        outs = [((rows, d), BF16), ((d, f), BF16), ((d, f), BF16), ((f, d), BF16)]
        dma = pltpu.SemaphoreType.DMA

        def buffers(n, r):
            shapes = ((2 * n, F32), (2 * n, BF16), (2 * n, BF16), (n, BF16), (n, BF16))
            return [pltpu.VMEM((m, r, d), t) for m, t in shapes]

        dx, *grads = pl.pallas_call(
            kernel,
            out_shape=[pltpu.VMEM(s, t) for s, t in outs],
            in_specs=[pl.BlockSpec(memory_space=pl.ANY)] * 7,
            out_specs=[pl.BlockSpec(memory_space=pltpu.VMEM)] * 4,
            scratch_shapes=[
                pltpu.VMEM((rows, d), BF16),
                pltpu.VMEM((rows, d + 2 * f), BF16),
                pltpu.VMEM((d, 2 * f), BF16),
                pltpu.VMEM((f, d), BF16),
                pltpu.VMEM((rows, 2 * f), BF16),
                pltpu.VMEM((rows, f), BF16),
                pltpu.VMEM((C, rows), BF16),
            ]
            + buffers(SMALL, RS)
            + buffers(nb, RB)
            + [
                pltpu.VMEM((RS, C), BF16),
                dma((7,)),
                dma((4,)),
                dma(()),
                dma((4 * (SMALL + nb),)),
                dma((SMALL + nb,)),
                dma((SMALL + nb,)),
                dma(()),
            ],
            compiler_params=pltpu.CompilerParams(
                collective_id=0, has_side_effects=True, vmem_limit_bytes=50 * 2**20
            ),
            name="block",
        )(x, dy, gate, up, w_gate, w_up, w_down)
        held, plain = pl.BlockSpec(memory_space=pltpu.VMEM), pl.BlockSpec(memory_space=pl.ANY)
        shapes = [jax.ShapeDtypeStruct(s, t) for s, t in outs]
        little = 2**20

        def pin(a):
            return pltpu.with_memory_space_constraint(a, pltpu.VMEM)

        dx, most, *grads = pl.pallas_call(
            write_most,
            out_shape=[pltpu.VMEM(*outs[0])] + shapes,
            in_specs=[plain] + [held] * 3,
            out_specs=[plain] * 5,
            scratch_shapes=[dma(())],
            input_output_aliases={0: 0},
            compiler_params=pltpu.CompilerParams(vmem_limit_bytes=little),
            name="write_most",
        )(pin(dx), *(pin(g) for g in grads))
        dx = pl.pallas_call(
            rest_kernel,
            out_shape=pltpu.VMEM(*outs[0]),
            in_specs=[plain],
            out_specs=plain,
            scratch_shapes=[
                dma((nb + SMALL - 2 + LAST,)), dma(()), pltpu.SemaphoreType.REGULAR, dma((2,)), dma(())
            ],
            input_output_aliases={0: 0},
            compiler_params=pltpu.CompilerParams(collective_id=1, has_side_effects=True, vmem_limit_bytes=little),
            name="rest",
        )(pin(dx))
        dx = pl.pallas_call(
            write_late,
            out_shape=shapes[0],
            in_specs=[held, plain],
            out_specs=plain,
            scratch_shapes=[dma(())],
            input_output_aliases={1: 0},
            compiler_params=pltpu.CompilerParams(vmem_limit_bytes=little),
            name="write_late",
        )(pin(dx), most)
        return dx, *grads

    tokens, columns, rows = P("dp", None), P(None, "tp"), P("tp", None)
    return jax.shard_map(
        step,
        mesh=mesh,
        in_specs=(tokens, tokens, P("dp", "tp"), P("dp", "tp"), columns, columns, rows),
        out_specs=(tokens, P("dp", "tp"), P("dp", "tp"), P(("dp", "tp"), None)),
        check_vma=False,
    )
```

profile of v0, /device:TPU:0, one launch (start us, length us, event | category | flops | bytes accessed | tf_op | source)
XLA Modules:
  0.0 54.9 jit_solution(18338353615480494691)
XLA Ops:
  0.6 45.8 %block.1 = (bf16[2048,1024]{1,0:T(8,128)(2,1)S(1)}, bf16[1024,768]{1,0:T(8,128)(2,1)S(1)}, bf16[1024,768]{1,0:T(8,128)(2,1)S(1)}, bf16[768,1024]{1,0:T(8,128)(2,1)S(1)}) custom-call(bf16[2048,1024]{1,0:T(8,128)(2,1)} %x_h.1, bf16[2048,1024]{1,0:T(8,128)(2,1)} %dy_h.1, bf16[2048,768]{1,0:T(8,128)(2,1)} %gate_h.1, bf16[2048,768]{1,0:T(8,128)(2,1)} %up_h.1, ...), custom_call_target="tpu_custom_call" | custom-call | tf_op jit(solution)/shard_map/block/pallas_call | solution.py:423
  46.4 3.2 %write_most.1 = (bf16[2048,1024]{1,0:T(8,128)(2,1)S(1)}, bf16[2048,1024]{1,0:T(8,128)(2,1)}, bf16[1024,768]{1,0:T(8,128)(2,1)}, bf16[1024,768]{1,0:T(8,128)(2,1)}, bf16[768,1024]{1,0:T(8,128)(2,1)}) custom-call(bf16[2048,1024]{1,0:T(8,128)(2,1)S(1)} %get-tuple-element.13.dx_v, ...), custom_call_target="tpu_custom_call", output_to_operand_aliasing={{0}: (0, {})} | custom-call | tf_op jit(solution)/shard_map/write_most/pallas_call | solution.py:461
  49.6 4.4 %rest.1.dx_v = bf16[2048,1024]{1,0:T(8,128)(2,1)S(1)} custom-call(bf16[2048,1024]{1,0:T(8,128)(2,1)S(1)} %get-tuple-element.17._), custom_call_target="tpu_custom_call", output_to_operand_aliasing={{}: (0, {})} | custom-call | tf_op jit(solution)/shard_map/rest/pallas_call | solution.py:471
  54.0 0.9 %write_late.1 = bf16[2048,1024]{1,0:T(8,128)(2,1)} custom-call(bf16[2048,1024]{1,0:T(8,128)(2,1)S(1)} %rest.1.dx_v, bf16[2048,1024]{1,0:T(8,128)(2,1)} %get-tuple-element.18._), custom_call_target="tpu_custom_call", output_to_operand_aliasing={{}: (1, {})} | custom-call | tf_op jit(solution)/shard_map/write_late/pallas_call | solution.py:483
where the time goes:
time: 55 us; the launch traced here: 54.9 us
  Pallas kernels  54.3 us (99%)
  between operations  0.66 us (1%)
    pallas_call x1, Pallas kernels, step(): pl.pallas_call(kernel, out_shape=[pltpu.VMEM(s, t) for s, t in outs], in_...  45.8 us
    pallas_call x1, Pallas kernels, step(): pl.pallas_call(rest_kernel, out_shape=pltpu.VMEM(*outs[0]), in_specs=[pla...  4.4 us
    pallas_call x1, Pallas kernels, step(): pl.pallas_call(write_most, out_shape=[pltpu.VMEM(*outs[0])] + shapes, in_...  3.21 us

commit v1 on v0

--- a/solution.py
+++ b/solution.py
@@ -331,10 +331,11 @@
 
     @pl.when(core == EARLY)
     def _():
-        for n in range(len(pieces)):
+        for n in range(end):
             final_copy(n).start()
         pl.semaphore_wait(ready, 2)
         direct_copy.start()
+        final_copy(end).start()
         for n in range(len(pieces)):
             final_copy(n).wait_recv()
             if n < end:

time: 55 us -> 54.8 us (level)
  no operation moved by 1% of the time
where the time goes in v1:
time: 54.8 us; the launch traced here: 54.7 us
  Pallas kernels  54.1 us (99%)
  between operations  0.66 us (1%)
    pallas_call x1, Pallas kernels, step(): pl.pallas_call(kernel, out_shape=[pltpu.VMEM(s, t) for s, t in outs], in_...  45.8 us
    pallas_call x1, Pallas kernels, step(): pl.pallas_call(rest_kernel, out_shape=pltpu.VMEM(*outs[0]), in_specs=[pla...  4.21 us
    pallas_call x1, Pallas kernels, step(): pl.pallas_call(write_most, out_shape=[pltpu.VMEM(*outs[0])] + shapes, in_...  3.21 us

profile of v1, /device:TPU:0, one launch (start us, length us, event | category | flops | bytes accessed | tf_op | source)
XLA Modules:
  0.0 54.7 jit_solution(13285538181815366974)
XLA Ops:
  0.6 45.8 %block.1 = (bf16[2048,1024]{1,0:T(8,128)(2,1)S(1)}, bf16[1024,768]{1,0:T(8,128)(2,1)S(1)}, bf16[1024,768]{1,0:T(8,128)(2,1)S(1)}, bf16[768,1024]{1,0:T(8,128)(2,1)S(1)}) custom-call(bf16[2048,1024]{1,0:T(8,128)(2,1)} %x_h.1, bf16[2048,1024]{1,0:T(8,128)(2,1)} %dy_h.1, bf16[2048,768]{1,0:T(8,128)(2,1)} %gate_h.1, bf16[2048,768]{1,0:T(8,128)(2,1)} %up_h.1, ...), custom_call_target="tpu_custom_call" | custom-call | tf_op jit(solution)/shard_map/block/pallas_call | solution.py:424
  46.4 3.2 %write_most.1 = (bf16[2048,1024]{1,0:T(8,128)(2,1)S(1)}, bf16[2048,1024]{1,0:T(8,128)(2,1)}, bf16[1024,768]{1,0:T(8,128)(2,1)}, bf16[1024,768]{1,0:T(8,128)(2,1)}, bf16[768,1024]{1,0:T(8,128)(2,1)}) custom-call(bf16[2048,1024]{1,0:T(8,128)(2,1)S(1)} %get-tuple-element.13.dx_v, ...), custom_call_target="tpu_custom_call", output_to_operand_aliasing={{0}: (0, {})} | custom-call | tf_op jit(solution)/shard_map/write_most/pallas_call | solution.py:462
  49.6 4.2 %rest.1.dx_v = bf16[2048,1024]{1,0:T(8,128)(2,1)S(1)} custom-call(bf16[2048,1024]{1,0:T(8,128)(2,1)S(1)} %get-tuple-element.17._), custom_call_target="tpu_custom_call", output_to_operand_aliasing={{}: (0, {})} | custom-call | tf_op jit(solution)/shard_map/rest/pallas_call | solution.py:472
  53.8 0.9 %write_late.1 = bf16[2048,1024]{1,0:T(8,128)(2,1)} custom-call(bf16[2048,1024]{1,0:T(8,128)(2,1)S(1)} %rest.1.dx_v, bf16[2048,1024]{1,0:T(8,128)(2,1)} %get-tuple-element.18._), custom_call_target="tpu_custom_call", output_to_operand_aliasing={{}: (1, {})} | custom-call | tf_op jit(solution)/shard_map/write_late/pallas_call | solution.py:484

commit v2 on v1

--- a/solution.py
+++ b/solution.py
@@ -11,7 +11,7 @@
 F32, BF16 = jnp.float32, jnp.bfloat16
 C = 256
 SMALL, RS, RB = 2, 64, 128
-EARLY, LAST = 1, 4
+EARLY, LAST = 1, (16, 24, 24)
 
 
 def dot_t(a, b):
@@ -287,19 +287,19 @@
         all_of(dx.at[0 : half // 2], sent.at[2]).wait()
 
 
-def rest_kernel(_, dx, recv, direct, ready, sent, landed):
+def rest_kernel(_, dx, recv, ready, sent, landed):
     half = dx.shape[0] // 2
     me = lax.axis_index("tp")
     chip, core = me // 2, me % 2
     partner, peer, across = chip * 2 + (1 - core), (1 - chip) * 2 + core, (1 - chip) * 2 + (1 - core)
     big = [(SMALL * 2 * RS + j * 2 * RB, RB, 0, RB) for j in range(1, (half - SMALL * 2 * RS) // (2 * RB))]
     small = [(j * 2 * RS, RS, 0, RS) for j in range(SMALL - 1)]
-    last = [((SMALL - 1) * 2 * RS, RS, n * RS // LAST, RS // LAST) for n in range(LAST)]
+    last = [((SMALL - 1) * 2 * RS, RS, sum(LAST[:n]), size) for n, size in enumerate(LAST)]
     pieces = big + small + last
 
     def rows(owner, piece):
         at, r, off, size = piece
-        return pl.ds(pl.multiple_of(owner * half + at + core * r + off, size), size)
+        return pl.ds(pl.multiple_of(owner * half + at + core * r + off, 8), size)
 
     def copy(r, send, recv, to):
         return pltpu.make_async_remote_copy(
@@ -307,18 +307,17 @@
         )
 
     def final_copy(n):
-        return copy(rows(chip, pieces[n]), sent.at[0], recv.at[n], peer)
+        return copy(rows(chip, pieces[n]), sent, recv.at[n], peer)
 
     def core_copy(n):
-        return copy(rows(1 - chip, pieces[n]), sent.at[1], landed, partner)
+        return copy(rows(1 - chip, pieces[n]), sent, landed, partner)
 
     end = len(pieces) - 1
-    direct_copy = copy(rows(chip, pieces[end]), sent.at[0], direct, across)
+    direct_copy = copy(rows(chip, pieces[end]), sent, landed, across)
 
     def all_of(n, sem):
         return pltpu.make_async_copy(dx.at[0:n], dx.at[0:n], sem)
 
-    size = pieces[end][3]
     passes = half // 2 - RB
     barrier = pltpu.get_barrier_semaphore()
 
@@ -340,9 +339,7 @@
             final_copy(n).wait_recv()
             if n < end:
                 core_copy(n).start()
-        all_of(passes + size, sent.at[0]).wait()
-        all_of(passes - size, sent.at[1]).wait()
-        all_of(passes, landed).wait()
+        all_of(2 * passes, sent).wait()
 
     @pl.when(core != EARLY)
     def _():
@@ -350,9 +347,9 @@
             pl.semaphore_signal(ready, inc=1, device_id={"tp": to}, device_id_type=MESH)
         for n in range(len(pieces)):
             core_copy(n).start()
-        all_of(passes, sent.at[1]).wait()
-        all_of(passes - size, landed).wait()
-        direct_copy.wait_recv()
+        all_of(passes, sent).wait()
+
+    all_of(passes, landed).wait()
 
 
 def start_all(pairs, sem):
@@ -475,7 +472,7 @@
             in_specs=[plain],
             out_specs=plain,
             scratch_shapes=[
-                dma((nb + SMALL - 2 + LAST,)), dma(()), pltpu.SemaphoreType.REGULAR, dma((2,)), dma(())
+                dma((nb + SMALL - 2 + len(LAST),)), pltpu.SemaphoreType.REGULAR, dma(()), dma(())
             ],
             input_output_aliases={0: 0},
             compiler_params=pltpu.CompilerParams(collective_id=1, has_side_effects=True, vmem_limit_bytes=little),

time: 54.8 us -> 54.7 us (level)
  no operation moved by 1% of the time
where the time goes in v2:
time: 54.7 us; the launch traced here: 54.6 us
  Pallas kernels  53.9 us (99%)
  between operations  0.66 us (1%)
    pallas_call x1, Pallas kernels, step(): pl.pallas_call(kernel, out_shape=[pltpu.VMEM(s, t) for s, t in outs], in_...  45.8 us
    pallas_call x1, Pallas kernels, step(): pl.pallas_call(rest_kernel, out_shape=pltpu.VMEM(*outs[0]), in_specs=[pla...  4.03 us
    pallas_call x1, Pallas kernels, step(): pl.pallas_call(write_most, out_shape=[pltpu.VMEM(*outs[0])] + shapes, in_...  3.21 us

profile of v2, /device:TPU:0, one launch (start us, length us, event | category | flops | bytes accessed | tf_op | source)
XLA Modules:
  0.0 54.6 jit_solution(13964710383031108004)
XLA Ops:
  0.6 45.8 %block.1 = (bf16[2048,1024]{1,0:T(8,128)(2,1)S(1)}, bf16[1024,768]{1,0:T(8,128)(2,1)S(1)}, bf16[1024,768]{1,0:T(8,128)(2,1)S(1)}, bf16[768,1024]{1,0:T(8,128)(2,1)S(1)}) custom-call(bf16[2048,1024]{1,0:T(8,128)(2,1)} %x_h.1, bf16[2048,1024]{1,0:T(8,128)(2,1)} %dy_h.1, bf16[2048,768]{1,0:T(8,128)(2,1)} %gate_h.1, bf16[2048,768]{1,0:T(8,128)(2,1)} %up_h.1, ...), custom_call_target="tpu_custom_call" | custom-call | tf_op jit(solution)/shard_map/block/pallas_call | solution.py:421
  46.4 3.2 %write_most.1 = (bf16[2048,1024]{1,0:T(8,128)(2,1)S(1)}, bf16[2048,1024]{1,0:T(8,128)(2,1)}, bf16[1024,768]{1,0:T(8,128)(2,1)}, bf16[1024,768]{1,0:T(8,128)(2,1)}, bf16[768,1024]{1,0:T(8,128)(2,1)}) custom-call(bf16[2048,1024]{1,0:T(8,128)(2,1)S(1)} %get-tuple-element.13.dx_v, ...), custom_call_target="tpu_custom_call", output_to_operand_aliasing={{0}: (0, {})} | custom-call | tf_op jit(solution)/shard_map/write_most/pallas_call | solution.py:459
  49.6 4.0 %rest.1.dx_v = bf16[2048,1024]{1,0:T(8,128)(2,1)S(1)} custom-call(bf16[2048,1024]{1,0:T(8,128)(2,1)S(1)} %get-tuple-element.17._), custom_call_target="tpu_custom_call", output_to_operand_aliasing={{}: (0, {})} | custom-call | tf_op jit(solution)/shard_map/rest/pallas_call | solution.py:469
  53.7 0.9 %write_late.1 = bf16[2048,1024]{1,0:T(8,128)(2,1)} custom-call(bf16[2048,1024]{1,0:T(8,128)(2,1)S(1)} %rest.1.dx_v, bf16[2048,1024]{1,0:T(8,128)(2,1)} %get-tuple-element.18._), custom_call_target="tpu_custom_call", output_to_operand_aliasing={{}: (1, {})} | custom-call | tf_op jit(solution)/shard_map/write_late/pallas_call | solution.py:481

commit v3 on v2

--- a/solution.py
+++ b/solution.py
@@ -140,7 +140,7 @@
             dx[r, :C] = (total[:, :C] + extra[...].astype(F32)).astype(BF16)
         else:
             dx[r, :] = total.astype(BF16)
-        if q is big and j == 0:
+        if j == 0:
             final_copy(q, j).start()
         else:
 
@@ -269,15 +269,15 @@
         def _():
             pass_on(big, 0)
 
-    ahead = RB
     all_of(dx.at[0:half], sent.at[0]).wait()
     all_of(dx.at[0 : half // 2], sent.at[1]).wait()
-    all_of(dx.at[0 : half // 2 + ahead], sent.at[3]).wait()
-    all_of(dx.at[0 : half // 2 + ahead], landed).wait()
 
     @pl.when(core == EARLY)
     def _():
-        all_of(dx.at[0:ahead], sent.at[2]).wait()
+        pass_on(small, 0)
+        all_of(dx.at[0 : RB + RS], sent.at[2]).wait()
+        all_of(dx.at[0 : half // 2 + RB + RS], sent.at[3]).wait()
+        all_of(dx.at[0 : half // 2 + RB], landed).wait()
 
     @pl.when(core != EARLY)
     def _():
@@ -285,6 +285,8 @@
             for j in range(1 if q is big else 0, q.n):
                 final_copy(q, j).wait_recv()
         all_of(dx.at[0 : half // 2], sent.at[2]).wait()
+        all_of(dx.at[0 : half // 2 + RB], sent.at[3]).wait()
+        all_of(dx.at[0 : half // 2 + RB + RS], landed).wait()
 
 
 def rest_kernel(_, dx, recv, ready, sent, landed):
@@ -293,7 +295,8 @@
     chip, core = me // 2, me % 2
     partner, peer, across = chip * 2 + (1 - core), (1 - chip) * 2 + core, (1 - chip) * 2 + (1 - core)
     big = [(SMALL * 2 * RS + j * 2 * RB, RB, 0, RB) for j in range(1, (half - SMALL * 2 * RS) // (2 * RB))]
-    small = [(j * 2 * RS, RS, 0, RS) for j in range(SMALL - 1)]
+    small = [(j * 2 * RS, RS, 0, RS) for j in range(1, SMALL - 1)]
+    here = (0, RS, 0, RS)
     last = [((SMALL - 1) * 2 * RS, RS, sum(LAST[:n]), size) for n, size in enumerate(LAST)]
     pieces = big + small + last
 
@@ -310,7 +313,7 @@
         return copy(rows(chip, pieces[n]), sent, recv.at[n], peer)
 
     def core_copy(n):
-        return copy(rows(1 - chip, pieces[n]), sent, landed, partner)
+        return copy(rows(1 - chip, here if n is None else pieces[n]), sent, landed, partner)
 
     end = len(pieces) - 1
     direct_copy = copy(rows(chip, pieces[end]), sent, landed, across)
@@ -318,7 +321,7 @@
     def all_of(n, sem):
         return pltpu.make_async_copy(dx.at[0:n], dx.at[0:n], sem)
 
-    passes = half // 2 - RB
+    passes = half // 2 - RB - RS
     barrier = pltpu.get_barrier_semaphore()
 
     @pl.when(core == EARLY)
@@ -340,16 +343,17 @@
             if n < end:
                 core_copy(n).start()
         all_of(2 * passes, sent).wait()
+        all_of(passes + RS, landed).wait()
 
     @pl.when(core != EARLY)
     def _():
         for to in (partner, across):
             pl.semaphore_signal(ready, inc=1, device_id={"tp": to}, device_id_type=MESH)
+        core_copy(None).start()
         for n in range(len(pieces)):
             core_copy(n).start()
-        all_of(passes, sent).wait()
-
-    all_of(passes, landed).wait()
+        all_of(passes + RS, sent).wait()
+        all_of(passes, landed).wait()
 
 
 def start_all(pairs, sem):
@@ -381,8 +385,8 @@
 
 
 def write_most(dx_v, dwg_v, dwu_v, dwd_v, _, dx, dwg, dwu, dwd, sem):
-    done, late, _ = rows_of(dx)
-    pairs = [(dx_v.at[r], dx.at[r]) for r in done]
+    done, late, early = rows_of(dx)
+    pairs = [(dx_v.at[r], dx.at[r]) for r in done + early[:1]]
     for src, dst in ((dwg_v, dwg), (dwu_v, dwu), (dwd_v, dwd)):
         n = src.shape[0] // 2
         pairs += [(src.at[r], dst.at[r]) for r in (pl.ds(0, n), pl.ds(n, n))]
@@ -397,7 +401,7 @@
 
 def write_late(dx_v, _, dx, sem):
     _, late, early = rows_of(dx)
-    copies = start_all([(dx_v.at[r], dx.at[r]) for r in early], sem)
+    copies = start_all([(dx_v.at[r], dx.at[r]) for r in early[1:]], sem)
 
     @pl.when(lax.rem(lax.axis_index("tp"), 2) == EARLY)
     def _():
@@ -472,7 +476,7 @@
             in_specs=[plain],
             out_specs=plain,
             scratch_shapes=[
-                dma((nb + SMALL - 2 + len(LAST),)), pltpu.SemaphoreType.REGULAR, dma(()), dma(())
+                dma((nb + SMALL - 3 + len(LAST),)), pltpu.SemaphoreType.REGULAR, dma(()), dma(())
             ],
             input_output_aliases={0: 0},
             compiler_params=pltpu.CompilerParams(collective_id=1, has_side_effects=True, vmem_limit_bytes=little),

time: 54.7 us -> 55 us (level)
    pallas_call x1, Pallas kernels: 45.8 us -> 46.5 us  [step(): pl.pallas_call(kernel, out_shape=[pltpu.VMEM(s, t) for s, t in outs], in_...]
where the time goes in v3:
time: 55 us; the launch traced here: 54.9 us
  Pallas kernels  54.2 us (99%)
  between operations  0.66 us (1%)
    pallas_call x1, Pallas kernels, step(): pl.pallas_call(kernel, out_shape=[pltpu.VMEM(s, t) for s, t in outs], in_...  46.5 us
    pallas_call x1, Pallas kernels, step(): pl.pallas_call(rest_kernel, out_shape=pltpu.VMEM(*outs[0]), in_specs=[pla...  3.63 us
    pallas_call x1, Pallas kernels, step(): pl.pallas_call(write_most, out_shape=[pltpu.VMEM(*outs[0])] + shapes, in_...  3.25 us

profile of v3, /device:TPU:0, one launch (start us, length us, event | category | flops | bytes accessed | tf_op | source)
XLA Modules:
  0.0 54.9 jit_solution(8845069573925053780)
XLA Ops:
  0.6 46.5 %block.1 = (bf16[2048,1024]{1,0:T(8,128)(2,1)S(1)}, bf16[1024,768]{1,0:T(8,128)(2,1)S(1)}, bf16[1024,768]{1,0:T(8,128)(2,1)S(1)}, bf16[768,1024]{1,0:T(8,128)(2,1)S(1)}) custom-call(bf16[2048,1024]{1,0:T(8,128)(2,1)} %x_h.1, bf16[2048,1024]{1,0:T(8,128)(2,1)} %dy_h.1, bf16[2048,768]{1,0:T(8,128)(2,1)} %gate_h.1, bf16[2048,768]{1,0:T(8,128)(2,1)} %up_h.1, ...), custom_call_target="tpu_custom_call" | custom-call | tf_op jit(solution)/shard_map/block/pallas_call | solution.py:425
  47.1 3.3 %write_most.1 = (bf16[2048,1024]{1,0:T(8,128)(2,1)S(1)}, bf16[2048,1024]{1,0:T(8,128)(2,1)}, bf16[1024,768]{1,0:T(8,128)(2,1)}, bf16[1024,768]{1,0:T(8,128)(2,1)}, bf16[768,1024]{1,0:T(8,128)(2,1)}) custom-call(bf16[2048,1024]{1,0:T(8,128)(2,1)S(1)} %get-tuple-element.13.dx_v, ...), custom_call_target="tpu_custom_call", output_to_operand_aliasing={{0}: (0, {})} | custom-call | tf_op jit(solution)/shard_map/write_most/pallas_call | solution.py:463
  50.4 3.6 %rest.1.dx_v = bf16[2048,1024]{1,0:T(8,128)(2,1)S(1)} custom-call(bf16[2048,1024]{1,0:T(8,128)(2,1)S(1)} %get-tuple-element.17._), custom_call_target="tpu_custom_call", output_to_operand_aliasing={{}: (0, {})} | custom-call | tf_op jit(solution)/shard_map/rest/pallas_call | solution.py:473
  54.0 0.9 %write_late.1 = bf16[2048,1024]{1,0:T(8,128)(2,1)} custom-call(bf16[2048,1024]{1,0:T(8,128)(2,1)S(1)} %rest.1.dx_v, bf16[2048,1024]{1,0:T(8,128)(2,1)} %get-tuple-element.18._), custom_call_target="tpu_custom_call", output_to_operand_aliasing={{}: (1, {})} | custom-call | tf_op jit(solution)/shard_map/write_late/pallas_call | solution.py:485

commit v4 on v2

--- a/solution.py
+++ b/solution.py
@@ -110,10 +110,13 @@
         for n in range(f // C):
             hidden_tile(q, e, n, dyb)
 
-    def term_tile(q, e, n, lhs):
+    def term_tile(q, e, n, lhs, alone=False):
         t = dot_t(lhs, wgu[tile(n), :])
         q.tsend[e, :, tile(n)] = t[: q.r].astype(BF16)
-        q.own[e, :, tile(n)] = t[q.r :]
+        if alone:
+            q.psend[e, :, tile(n)] = t[q.r :].astype(BF16)
+        else:
+            q.own[e, :, tile(n)] = t[q.r :]
 
     def term_part(q, e):
         lhs = both(dgu, q, e)
@@ -198,10 +201,9 @@
             if q is small and e == 0:
                 all_of(wgu.at[halves[n]], load_sem.at[gu + n]).wait()
             for m in range(nd // 2):
-                term_tile(q, e, n * (nd // 2) + m, lhs)
+                term_tile(q, e, n * (nd // 2) + m, lhs, alone=q is small and e == 0 and n == 0 and m == 0)
             cols = halves[n]
             if q is small and e == 0 and n == 0:
-                psend_s[0, :, tile(0)] = own_s[0, :, tile(0)].astype(BF16)
                 part_copy(small, 0, tile(0)).start()
                 extra_copy().start()
                 cols = rest_cols

time: 54.7 us -> 54.7 us (level)
  no operation moved by 1% of the time
where the time goes in v4:
time: 54.7 us; the launch traced here: 54.6 us
  Pallas kernels  53.9 us (99%)
  between operations  0.66 us (1%)
    pallas_call x1, Pallas kernels, step(): pl.pallas_call(kernel, out_shape=[pltpu.VMEM(s, t) for s, t in outs], in_...  45.8 us
    pallas_call x1, Pallas kernels, step(): pl.pallas_call(rest_kernel, out_shape=pltpu.VMEM(*outs[0]), in_specs=[pla...  4.03 us
    pallas_call x1, Pallas kernels, step(): pl.pallas_call(write_most, out_shape=[pltpu.VMEM(*outs[0])] + shapes, in_...  3.21 us

profile of v4, /device:TPU:0, one launch (start us, length us, event | category | flops | bytes accessed | tf_op | source)
XLA Modules:
  0.0 54.6 jit_solution(13964710383031108004)
XLA Ops:
  0.6 45.8 %block.1 = (bf16[2048,1024]{1,0:T(8,128)(2,1)S(1)}, bf16[1024,768]{1,0:T(8,128)(2,1)S(1)}, bf16[1024,768]{1,0:T(8,128)(2,1)S(1)}, bf16[768,1024]{1,0:T(8,128)(2,1)S(1)}) custom-call(bf16[2048,1024]{1,0:T(8,128)(2,1)} %x_h.1, bf16[2048,1024]{1,0:T(8,128)(2,1)} %dy_h.1, bf16[2048,768]{1,0:T(8,128)(2,1)} %gate_h.1, bf16[2048,768]{1,0:T(8,128)(2,1)} %up_h.1, ...), custom_call_target="tpu_custom_call" | custom-call | tf_op jit(solution)/shard_map/block/pallas_call | solution.py:423
  46.4 3.2 %write_most.1 = (bf16[2048,1024]{1,0:T(8,128)(2,1)S(1)}, bf16[2048,1024]{1,0:T(8,128)(2,1)}, bf16[1024,768]{1,0:T(8,128)(2,1)}, bf16[1024,768]{1,0:T(8,128)(2,1)}, bf16[768,1024]{1,0:T(8,128)(2,1)}) custom-call(bf16[2048,1024]{1,0:T(8,128)(2,1)S(1)} %get-tuple-element.13.dx_v, ...), custom_call_target="tpu_custom_call", output_to_operand_aliasing={{0}: (0, {})} | custom-call | tf_op jit(solution)/shard_map/write_most/pallas_call | solution.py:461
  49.6 4.0 %rest.1.dx_v = bf16[2048,1024]{1,0:T(8,128)(2,1)S(1)} custom-call(bf16[2048,1024]{1,0:T(8,128)(2,1)S(1)} %get-tuple-element.17._), custom_call_target="tpu_custom_call", output_to_operand_aliasing={{}: (0, {})} | custom-call | tf_op jit(solution)/shard_map/rest/pallas_call | solution.py:471
  53.7 0.9 %write_late.1 = bf16[2048,1024]{1,0:T(8,128)(2,1)} custom-call(bf16[2048,1024]{1,0:T(8,128)(2,1)S(1)} %rest.1.dx_v, bf16[2048,1024]{1,0:T(8,128)(2,1)} %get-tuple-element.18._), custom_call_target="tpu_custom_call", output_to_operand_aliasing={{}: (1, {})} | custom-call | tf_op jit(solution)/shard_map/write_late/pallas_call | solution.py:483

commit v5 on v4

--- a/solution.py
+++ b/solution.py
@@ -171,9 +171,9 @@
             dwd[r, tile(n)] = dot(xt[...], dyv[:, tile(n)]).astype(BF16)
 
     nf, nd = f // C, d // C
-    w_sem, first_rows, gu, second_rows, rest, x_sem = 0, 1, 2, 4, 5, 6
+    w_sem, first_rows, gu, second_rows, rest, x_sem = 0, 2, 3, 5, 6, 7
     first = load(small, 0, first_rows)
-    wds = [local(wd_h.at[tile(n)], wd.at[tile(n)], w_sem) for n in range(nf)]
+    wds = [local(wd_h.at[tile(n)], wd.at[tile(n)], w_sem + min(n, 1)) for n in range(nf)]
     start(first[:1] + wds[:1] + first[1:] + wds[1:])
     for n in range(nd):
         start([local(w.at[tile(n)], wgu.at[tile(n), c * f : (c + 1) * f], gu + n // 2) for c, w in enumerate((wg_h, wu_h))])
@@ -190,8 +190,12 @@
         pl.semaphore_signal(barrier, inc=1, device_id={"tp": to}, device_id_type=MESH)
 
     all_of(acts.at[pl.ds(base(small, 0), 2 * RS)], load_sem.at[first_rows]).wait()
-    all_of(wd, load_sem.at[w_sem]).wait()
-    hidden_part(small, 0)
+    wds[0].wait()
+    dyb = both(dyv, small, 0)
+    hidden_tile(small, 0, 0, dyb)
+    all_of(wd.at[C:f], load_sem.at[w_sem + 1]).wait()
+    for n in range(1, nf):
+        hidden_tile(small, 0, n, dyb)
     pl.semaphore_wait(barrier, 3)
     halves = [slice(n * (d // 2), (n + 1) * (d // 2)) for n in range(2)]
 
@@ -309,7 +313,7 @@
         )
 
     def final_copy(n):
-        return copy(rows(chip, pieces[n]), sent, recv.at[n], peer)
+        return copy(rows(chip, pieces[n]), sent, recv.at[max(n - len(big) + 1, 0)], peer)
 
     def core_copy(n):
         return copy(rows(1 - chip, pieces[n]), sent, landed, partner)
@@ -338,7 +342,10 @@
         direct_copy.start()
         final_copy(end).start()
         for n in range(len(pieces)):
-            final_copy(n).wait_recv()
+            if n == 0:
+                all_of(len(big) * RB, recv.at[0]).wait()
+            elif n >= len(big):
+                final_copy(n).wait_recv()
             if n < end:
                 core_copy(n).start()
         all_of(2 * passes, sent).wait()
@@ -438,7 +445,7 @@
             + buffers(nb, RB)
             + [
                 pltpu.VMEM((RS, C), BF16),
-                dma((7,)),
+                dma((8,)),
                 dma((4,)),
                 dma(()),
                 dma((4 * (SMALL + nb),)),
@@ -474,7 +481,7 @@
             in_specs=[plain],
             out_specs=plain,
             scratch_shapes=[
-                dma((nb + SMALL - 2 + len(LAST),)), pltpu.SemaphoreType.REGULAR, dma(()), dma(())
+                dma((SMALL + len(LAST),)), pltpu.SemaphoreType.REGULAR, dma(()), dma(())
             ],
             input_output_aliases={0: 0},
             compiler_params=pltpu.CompilerParams(collective_id=1, has_side_effects=True, vmem_limit_bytes=little),

time: 54.7 us -> 54.5 us (level)
  no operation moved by 1% of the time
where the time goes in v5:
time: 54.5 us; the launch traced here: 54.4 us
  Pallas kernels  53.7 us (99%)
  between operations  0.66 us (1%)
    pallas_call x1, Pallas kernels, step(): pl.pallas_call(kernel, out_shape=[pltpu.VMEM(s, t) for s, t in outs], in_...  45.6 us
    pallas_call x1, Pallas kernels, step(): pl.pallas_call(rest_kernel, out_shape=pltpu.VMEM(*outs[0]), in_specs=[pla...  4.02 us
    pallas_call x1, Pallas kernels, step(): pl.pallas_call(write_most, out_shape=[pltpu.VMEM(*outs[0])] + shapes, in_...  3.21 us

profile of v5, /device:TPU:0, one launch (start us, length us, event | category | flops | bytes accessed | tf_op | source)
XLA Modules:
  0.0 54.4 jit_solution(7738393419920147340)
XLA Ops:
  0.6 45.6 %block.1 = (bf16[2048,1024]{1,0:T(8,128)(2,1)S(1)}, bf16[1024,768]{1,0:T(8,128)(2,1)S(1)}, bf16[1024,768]{1,0:T(8,128)(2,1)S(1)}, bf16[768,1024]{1,0:T(8,128)(2,1)S(1)}) custom-call(bf16[2048,1024]{1,0:T(8,128)(2,1)} %x_h.1, bf16[2048,1024]{1,0:T(8,128)(2,1)} %dy_h.1, bf16[2048,768]{1,0:T(8,128)(2,1)} %gate_h.1, bf16[2048,768]{1,0:T(8,128)(2,1)} %up_h.1, ...), custom_call_target="tpu_custom_call" | custom-call | tf_op jit(solution)/shard_map/block/pallas_call | solution.py:430
  46.2 3.2 %write_most.1 = (bf16[2048,1024]{1,0:T(8,128)(2,1)S(1)}, bf16[2048,1024]{1,0:T(8,128)(2,1)}, bf16[1024,768]{1,0:T(8,128)(2,1)}, bf16[1024,768]{1,0:T(8,128)(2,1)}, bf16[768,1024]{1,0:T(8,128)(2,1)}) custom-call(bf16[2048,1024]{1,0:T(8,128)(2,1)S(1)} %get-tuple-element.13.dx_v, ...), custom_call_target="tpu_custom_call", output_to_operand_aliasing={{0}: (0, {})} | custom-call | tf_op jit(solution)/shard_map/write_most/pallas_call | solution.py:468
  49.4 4.0 %rest.1.dx_v = bf16[2048,1024]{1,0:T(8,128)(2,1)S(1)} custom-call(bf16[2048,1024]{1,0:T(8,128)(2,1)S(1)} %get-tuple-element.17._), custom_call_target="tpu_custom_call", output_to_operand_aliasing={{}: (0, {})} | custom-call | tf_op jit(solution)/shard_map/rest/pallas_call | solution.py:478
  53.5 0.9 %write_late.1 = bf16[2048,1024]{1,0:T(8,128)(2,1)} custom-call(bf16[2048,1024]{1,0:T(8,128)(2,1)S(1)} %rest.1.dx_v, bf16[2048,1024]{1,0:T(8,128)(2,1)} %get-tuple-element.18._), custom_call_target="tpu_custom_call", output_to_operand_aliasing={{}: (1, {})} | custom-call | tf_op jit(solution)/shard_map/write_late/pallas_call | solution.py:490

commit v6 on v5

--- a/solution.py
+++ b/solution.py
@@ -172,9 +172,14 @@
 
     nf, nd = f // C, d // C
     w_sem, first_rows, gu, second_rows, rest, x_sem = 0, 2, 3, 5, 6, 7
-    first = load(small, 0, first_rows)
+    now = pl.ds(base(small, 0), 2 * RS)
+    first = [local(dy_h.at[now], dyv.at[now], first_rows)]
+    later = []
+    for src, dst in ((gate_h, gv), (up_h, uv)):
+        first.append(local(src.at[now, 0:C], dst.at[now, 0:C], first_rows))
+        later.append(local(src.at[now, C:f], dst.at[now, C:f], w_sem + 1))
     wds = [local(wd_h.at[tile(n)], wd.at[tile(n)], w_sem + min(n, 1)) for n in range(nf)]
-    start(first[:1] + wds[:1] + first[1:] + wds[1:])
+    start(first[:1] + wds[:1] + first[1:] + wds[1:] + later)
     for n in range(nd):
         start([local(w.at[tile(n)], wgu.at[tile(n), c * f : (c + 1) * f], gu + n // 2) for c, w in enumerate((wg_h, wu_h))])
     start(load(small, 1, second_rows))
@@ -189,11 +194,12 @@
     for to in (partner, peer, across):
         pl.semaphore_signal(barrier, inc=1, device_id={"tp": to}, device_id_type=MESH)
 
-    all_of(acts.at[pl.ds(base(small, 0), 2 * RS)], load_sem.at[first_rows]).wait()
+    all_of(acts.at[now, 0 : d + 2 * C], load_sem.at[first_rows]).wait()
     wds[0].wait()
     dyb = both(dyv, small, 0)
     hidden_tile(small, 0, 0, dyb)
-    all_of(wd.at[C:f], load_sem.at[w_sem + 1]).wait()
+    more = 2 * RS * 2 * (f - C) // d
+    all_of(xv.at[0 : f - C + more], load_sem.at[w_sem + 1]).wait()
     for n in range(1, nf):
         hidden_tile(small, 0, n, dyb)
     pl.semaphore_wait(barrier, 3)

time: 54.5 us -> 54.4 us (level)
  no operation moved by 1% of the time
where the time goes in v6:
time: 54.4 us
  Pallas kernels  53.7 us (99%)
  between operations  0.66 us (1%)
    pallas_call x1, Pallas kernels, step(): pl.pallas_call(kernel, out_shape=[pltpu.VMEM(s, t) for s, t in outs], in_...  45.6 us
    pallas_call x1, Pallas kernels, step(): pl.pallas_call(rest_kernel, out_shape=pltpu.VMEM(*outs[0]), in_specs=[pla...  4.02 us
    pallas_call x1, Pallas kernels, step(): pl.pallas_call(write_most, out_shape=[pltpu.VMEM(*outs[0])] + shapes, in_...  3.21 us

profile of v6, /device:TPU:0, one launch (start us, length us, event | category | flops | bytes accessed | tf_op | source)
XLA Modules:
  0.0 54.4 jit_solution(16703446585758980337)
XLA Ops:
  0.6 45.6 %block.1 = (bf16[2048,1024]{1,0:T(8,128)(2,1)S(1)}, bf16[1024,768]{1,0:T(8,128)(2,1)S(1)}, bf16[1024,768]{1,0:T(8,128)(2,1)S(1)}, bf16[768,1024]{1,0:T(8,128)(2,1)S(1)}) custom-call(bf16[2048,1024]{1,0:T(8,128)(2,1)} %x_h.1, bf16[2048,1024]{1,0:T(8,128)(2,1)} %dy_h.1, bf16[2048,768]{1,0:T(8,128)(2,1)} %gate_h.1, bf16[2048,768]{1,0:T(8,128)(2,1)} %up_h.1, ...), custom_call_target="tpu_custom_call" | custom-call | tf_op jit(solution)/shard_map/block/pallas_call | solution.py:436
  46.2 3.2 %write_most.1 = (bf16[2048,1024]{1,0:T(8,128)(2,1)S(1)}, bf16[2048,1024]{1,0:T(8,128)(2,1)}, bf16[1024,768]{1,0:T(8,128)(2,1)}, bf16[1024,768]{1,0:T(8,128)(2,1)}, bf16[768,1024]{1,0:T(8,128)(2,1)}) custom-call(bf16[2048,1024]{1,0:T(8,128)(2,1)S(1)} %get-tuple-element.13.dx_v, ...), custom_call_target="tpu_custom_call", output_to_operand_aliasing={{0}: (0, {})} | custom-call | tf_op jit(solution)/shard_map/write_most/pallas_call | solution.py:474
  49.4 4.0 %rest.1.dx_v = bf16[2048,1024]{1,0:T(8,128)(2,1)S(1)} custom-call(bf16[2048,1024]{1,0:T(8,128)(2,1)S(1)} %get-tuple-element.17._), custom_call_target="tpu_custom_call", output_to_operand_aliasing={{}: (0, {})} | custom-call | tf_op jit(solution)/shard_map/rest/pallas_call | solution.py:484
  53.4 0.9 %write_late.1 = bf16[2048,1024]{1,0:T(8,128)(2,1)} custom-call(bf16[2048,1024]{1,0:T(8,128)(2,1)S(1)} %rest.1.dx_v, bf16[2048,1024]{1,0:T(8,128)(2,1)} %get-tuple-element.18._), custom_call_target="tpu_custom_call", output_to_operand_aliasing={{}: (1, {})} | custom-call | tf_op jit(solution)/shard_map/write_late/pallas_call | solution.py:496

commit v7 on v6

--- a/solution.py
+++ b/solution.py
@@ -202,7 +202,6 @@
     all_of(xv.at[0 : f - C + more], load_sem.at[w_sem + 1]).wait()
     for n in range(1, nf):
         hidden_tile(small, 0, n, dyb)
-    pl.semaphore_wait(barrier, 3)
     halves = [slice(n * (d // 2), (n + 1) * (d // 2)) for n in range(2)]
 
     def halves_of_term(q, e):
@@ -214,6 +213,7 @@
                 term_tile(q, e, n * (nd // 2) + m, lhs, alone=q is small and e == 0 and n == 0 and m == 0)
             cols = halves[n]
             if q is small and e == 0 and n == 0:
+                pl.semaphore_wait(barrier, 3)
                 part_copy(small, 0, tile(0)).start()
                 extra_copy().start()
                 cols = rest_cols

time: 54.4 us -> 54.5 us (level)
  no operation moved by 1% of the time
where the time goes in v7:
time: 54.5 us; the launch traced here: 54.4 us
  Pallas kernels  53.7 us (99%)
  between operations  0.66 us (1%)
    pallas_call x1, Pallas kernels, step(): pl.pallas_call(kernel, out_shape=[pltpu.VMEM(s, t) for s, t in outs], in_...  45.6 us
    pallas_call x1, Pallas kernels, step(): pl.pallas_call(rest_kernel, out_shape=pltpu.VMEM(*outs[0]), in_specs=[pla...  4.02 us
    pallas_call x1, Pallas kernels, step(): pl.pallas_call(write_most, out_shape=[pltpu.VMEM(*outs[0])] + shapes, in_...  3.21 us

profile of v7, /device:TPU:0, one launch (start us, length us, event | category | flops | bytes accessed | tf_op | source)
XLA Modules:
  0.0 54.4 jit_solution(4752721530657198849)
XLA Ops:
  0.6 45.6 %block.1 = (bf16[2048,1024]{1,0:T(8,128)(2,1)S(1)}, bf16[1024,768]{1,0:T(8,128)(2,1)S(1)}, bf16[1024,768]{1,0:T(8,128)(2,1)S(1)}, bf16[768,1024]{1,0:T(8,128)(2,1)S(1)}) custom-call(bf16[2048,1024]{1,0:T(8,128)(2,1)} %x_h.1, bf16[2048,1024]{1,0:T(8,128)(2,1)} %dy_h.1, bf16[2048,768]{1,0:T(8,128)(2,1)} %gate_h.1, bf16[2048,768]{1,0:T(8,128)(2,1)} %up_h.1, ...), custom_call_target="tpu_custom_call" | custom-call | tf_op jit(solution)/shard_map/block/pallas_call | solution.py:436
  46.2 3.2 %write_most.1 = (bf16[2048,1024]{1,0:T(8,128)(2,1)S(1)}, bf16[2048,1024]{1,0:T(8,128)(2,1)}, bf16[1024,768]{1,0:T(8,128)(2,1)}, bf16[1024,768]{1,0:T(8,128)(2,1)}, bf16[768,1024]{1,0:T(8,128)(2,1)}) custom-call(bf16[2048,1024]{1,0:T(8,128)(2,1)S(1)} %get-tuple-element.13.dx_v, ...), custom_call_target="tpu_custom_call", output_to_operand_aliasing={{0}: (0, {})} | custom-call | tf_op jit(solution)/shard_map/write_most/pallas_call | solution.py:474
  49.4 4.0 %rest.1.dx_v = bf16[2048,1024]{1,0:T(8,128)(2,1)S(1)} custom-call(bf16[2048,1024]{1,0:T(8,128)(2,1)S(1)} %get-tuple-element.17._), custom_call_target="tpu_custom_call", output_to_operand_aliasing={{}: (0, {})} | custom-call | tf_op jit(solution)/shard_map/rest/pallas_call | solution.py:484
  53.5 0.9 %write_late.1 = bf16[2048,1024]{1,0:T(8,128)(2,1)} custom-call(bf16[2048,1024]{1,0:T(8,128)(2,1)S(1)} %rest.1.dx_v, bf16[2048,1024]{1,0:T(8,128)(2,1)} %get-tuple-element.18._), custom_call_target="tpu_custom_call", output_to_operand_aliasing={{}: (1, {})} | custom-call | tf_op jit(solution)/shard_map/write_late/pallas_call | solution.py:496
